TPU v7x, 32 devices: a whole 2x2x4 slice. The times are simulated.
32 devices in a mesh: basin: 2 (over x), recv: 8 (over z, y), src: 2 (over core).
Axes of the slice: x: 2, y: 2, z: 4, core: 2. Of those that a mesh axis runs over, the one named last changes fastest.
Arguments:
- positions: float32 [3, 4096], P(None, ('basin', 'recv', 'src')), parts along dimension 1, may hold values from -1.1 to 1.1, as said below
- normals: float32 [3, 4096], P(None, ('basin', 'recv', 'src')), parts along dimension 1, may hold values from -1 to 1, as said below
- area: float32 [4096], P(('basin', 'recv', 'src')), parts along dimension 0, may hold values from 0.0009765625 to 0.0078125
- albedo: float32 [4096], P(('basin', 'recv', 'src')), parts along dimension 0, may hold values from 0.1 to 0.6
- conductivity: float32 [4096], P(('basin', 'recv', 'src')), parts along dimension 0, may hold values from 0.05 to 0.4
- soil: float32 [32, 4096], P(None, ('basin', 'recv', 'src')), parts along dimension 1, may hold values from 0.5 to 1.2
- sun_tan: float32 [16], replicated, may hold values from 0.05 to 2
- samples: int32 [32, 32], P(('basin', 'recv', 'src')), parts along dimension 0, may hold values from 1 to 2047
- occupancy: int32 [32, 16], P('basin'), parts along dimension 0, may hold values 0 or 1
Outputs:
- soil_final: float32 [32, 4096], P(None, ('basin', 'recv', 'src')), parts along dimension 1
- bounce: float32 [16, 4096], P(None, ('basin', 'recv', 'src')), parts along dimension 1
There are 2 independent parts, one for each index of `basin`. A program takes and returns all parts, laid end to end along the dimension named above; an argument that names none is the same for every part. Nothing has to cross between parts.
Inputs may be any that keep to these rules, and one draw needn't show every extreme that they name: `positions`: facets lie on a bowl below z = 0. `normals`: each column has unit length.
All inputs are finite; a program needn't handle non-finite values.
Results may differ from a plain program's by a relative error of at most 0.0003.
Values may be sent and summed in bfloat16 or wider, within the bound.
A program may use at most 64 MiB of HBM per device.

v0:
```python
import math
import jax
import jax.numpy as jnp
from jax import lax
from jax.sharding import PartitionSpec as P

solar_flux = 2.0
emissivity = 0.9
surface_gain = 0.1
shade_width = 0.1
reach_offset = 0.05


def partner(value, axis, apart):
    mask = 2**apart
    pairs = [(source, source ^ mask) for source in range(lax.axis_size(axis))]
    return lax.ppermute(value, axis, pairs)


def fourth(value):
    square = value * value
    return square * square


def rotate(values, shift):
    count = values.shape[0]
    doubled = jnp.concatenate([values, values], 0)
    return lax.dynamic_slice_in_dim(doubled, shift, count, 0)


def profile_max(coords, offsets):
    px, py, pz = (coords[0], coords[1], coords[2])
    count = px.shape[0]

    def sweep(best, shift):
        delta_x = rotate(px, shift) - px
        delta_y = rotate(py, shift) - py
        reach = jnp.sqrt(delta_x * delta_x + delta_y * delta_y) + reach_offset
        slope = (rotate(pz, shift) - pz) / reach
        return (jnp.maximum(best, slope), None)

    start = jnp.full((count,), -1e30, jnp.float32)
    best, unused = lax.scan(sweep, start, offsets)
    return best


def horizons(coords, samples):
    return lax.map(lambda offsets: profile_max(coords, offsets), samples)


def sunlight(facing, sun_tan, horizon):
    count = sun_tan.shape[0]
    angle = 2.0 * math.pi * jnp.arange(count, dtype=jnp.float32) / count
    elevation = jnp.arctan(sun_tan)
    sun_x = jnp.cos(elevation) * jnp.cos(angle)
    sun_y = jnp.cos(elevation) * jnp.sin(angle)
    sun_z = jnp.sin(elevation)
    incidence = (
        sun_x[:, None] * facing[0][None, :]
        + sun_y[:, None] * facing[1][None, :]
        + sun_z[:, None] * facing[2][None, :]
    )
    shade = jax.nn.sigmoid((sun_tan[:, None] - horizon) / shade_width)
    return solar_flux * jnp.maximum(incidence, 0.0) * shade


def conduct(soil, direct, bounce, albedo, conductivity):

    def advance(temps, inputs):
        light, scattered = inputs
        grad = temps[1:] - temps[:-1]
        edge = jnp.zeros((1, temps.shape[1]), jnp.float32)
        change = jnp.concatenate([grad, edge], 0) - jnp.concatenate([edge, grad], 0)
        temps = temps + conductivity[None, :] * change
        absorbed = (1.0 - albedo) * (light + scattered)
        top = temps[0] + surface_gain * (absorbed - emissivity * fourth(temps[0]))
        return (jnp.concatenate([top[None, :], temps[1:]], 0), None)

    final, unused = lax.scan(advance, soil, (direct, bounce))
    return final


def view_tile(src_pos, src_nrm, src_area, src_ids, rec_pos, rec_nrm, mask_rows, width):
    onehot = (src_ids[:, None] == jnp.arange(mask_rows.shape[1], dtype=jnp.int32)[None, :]).astype(
        jnp.float32
    )
    weight = jnp.dot(
        onehot, mask_rows.T, preferred_element_type=jnp.float32, precision=lax.Precision.HIGHEST
    )
    weight = jnp.repeat(weight, width, axis=1)
    delta_x = src_pos[0][:, None] - rec_pos[0][None, :]
    delta_y = src_pos[1][:, None] - rec_pos[1][None, :]
    delta_z = src_pos[2][:, None] - rec_pos[2][None, :]
    facing = jnp.maximum(
        rec_nrm[0][None, :] * delta_x
        + rec_nrm[1][None, :] * delta_y
        + rec_nrm[2][None, :] * delta_z,
        0.0,
    )
    toward = jnp.maximum(
        -(
            src_nrm[0][:, None] * delta_x
            + src_nrm[1][:, None] * delta_y
            + src_nrm[2][:, None] * delta_z
        ),
        0.0,
    )
    spread = delta_x * delta_x + delta_y * delta_y + delta_z * delta_z + src_area[:, None]
    return (facing * toward * src_area[:, None] * weight / (math.pi * spread * spread)).astype(
        jnp.bfloat16
    )


def make_fold(src_pos, src_nrm, src_area, block_of, rec_pos, rec_nrm, mask_rows, width):

    def add_tile(carry, segment, begin, count):
        ids = block_of(begin + jnp.arange(count, dtype=jnp.int32))
        pos = lax.dynamic_slice_in_dim(src_pos, begin, count, 1)
        nrm = lax.dynamic_slice_in_dim(src_nrm, begin, count, 1)
        sizes = lax.dynamic_slice_in_dim(src_area, begin, count, 0)
        view = view_tile(pos, nrm, sizes, ids, rec_pos, rec_nrm, mask_rows, width)
        return carry + jnp.dot(segment, view, preferred_element_type=jnp.float32)

    def fold(carry, piece, start):
        count = piece.shape[1]

        def step_once(total, number):
            offset = number * width
            segment = lax.dynamic_slice_in_dim(piece, offset, width, 1)
            return (add_tile(total, segment, offset, width), None)

        total, unused = lax.scan(step_once, carry, jnp.arange(count // width, dtype=jnp.int32))
        return total

    return fold


def body(positions, normals, area, albedo, conductivity, soil, sun_tan, samples, occupancy):
    width = positions.shape[1]
    n_recv = lax.axis_size("recv")
    n_src = lax.axis_size("src")
    recv_index = lax.axis_index("recv")
    src_index = lax.axis_index("src")
    all_pos, all_nrm, all_area = (
        lax.all_gather(positions, ("recv", "src"), axis=1, tiled=True),
        lax.all_gather(normals, ("recv", "src"), axis=1, tiled=True),
        lax.all_gather(area, ("recv", "src"), axis=0, tiled=True),
    )
    horizon = horizons(all_pos, samples)
    facet_horizon = lax.all_to_all(
        horizon.astype(jnp.bfloat16), ("recv", "src"), split_axis=1, concat_axis=0, tiled=True
    ).astype(horizon.dtype)
    direct = sunlight(normals, sun_tan, facet_horizon)
    radiance = (albedo[None, :] * direct + emissivity * fourth(soil[0])[None, :]).astype(
        jnp.bfloat16
    )
    epochs = radiance.shape[0]
    table = occupancy.astype(jnp.float32)
    low_bits = recv_index % 4
    high_bits = recv_index // 4
    share = 4 * n_src
    rec_pos = lax.dynamic_slice_in_dim(all_pos, high_bits * share * width, share * width, 1)
    rec_nrm = lax.dynamic_slice_in_dim(all_nrm, high_bits * share * width, share * width, 1)
    mask_rows = lax.dynamic_slice_in_dim(table, high_bits * share, share, 0)
    column = low_bits * n_src + src_index

    def pick_class(values):
        lead = values.shape[:-1]
        arranged = values.reshape(lead + (n_recv // 4, share * width))
        chosen = lax.dynamic_slice_in_dim(arranged, column * width, width, len(lead) + 1)
        return chosen.reshape(lead + (n_recv // 4 * width,))

    def block_class(index):
        return index // width * share + column

    fold = make_fold(
        pick_class(all_pos),
        pick_class(all_nrm),
        pick_class(all_area),
        block_class,
        rec_pos,
        rec_nrm,
        mask_rows,
        width,
    )
    gathered = radiance
    for bit in range(2, n_recv.bit_length() - 1):
        other = partner(gathered, "recv", bit)
        upper = recv_index // (1 << bit) % 2 == 1
        gathered = jnp.where(
            upper, jnp.concatenate([other, gathered], 1), jnp.concatenate([gathered, other], 1)
        )
    start_sum = jnp.zeros((epochs, share * width), jnp.float32)
    partial_flux = fold(start_sum, gathered, jnp.int32(0))
    paired = lax.psum_scatter(
        partial_flux.reshape(epochs, 4, n_src, width), "src", scatter_dimension=2, tiled=True
    )
    paired = paired.reshape(epochs, 4, width)
    for bit in (1, 0):
        half = paired.shape[1] // 2
        lower = paired[:, :half]
        higher = paired[:, half:]
        upper = recv_index // (1 << bit) % 2 == 1
        keep = jnp.where(upper, higher, lower)
        outgoing = jnp.where(upper, lower, higher)
        paired = keep + partner(outgoing, "recv", bit)
    bounce = paired.reshape(epochs, width)
    final = conduct(soil, direct, bounce, albedo, conductivity)
    return (final, bounce)


def solution(mesh):
    in_specs = (
        P(None, ("basin", "recv", "src")),
        P(None, ("basin", "recv", "src")),
        P(("basin", "recv", "src")),
        P(("basin", "recv", "src")),
        P(("basin", "recv", "src")),
        P(None, ("basin", "recv", "src")),
        P(),
        P(("basin", "recv", "src"), None),
        P("basin", None),
    )
    out_specs = (P(None, ("basin", "recv", "src")), P(None, ("basin", "recv", "src")))
    return jax.shard_map(body, mesh=mesh, in_specs=in_specs, out_specs=out_specs, check_vma=False)
```

profile of v0, /device:TPU:0, one launch (start us, length us, event | category | flops | bytes accessed | tf_op | source)
XLA Modules:
  0.0 205.7 jit_solution(17961653555139462512)
XLA Ops:
  7.2 0.7 copy.50
  7.9 0.7 copy-done.6
  8.6 23.2 %all_gather.9 = f32[3,2048]{1,0:T(4,128)S(1)} all-gather(f32[3,128]{1,0:T(4,128)S(1)} %copy-done.6), channel_id=1, replica_groups=mesh['basin'=2,'recv'=8,'src'=2] {'recv','src'}, dimensions={1}, use_global_device_ids=true | all-gather | bytes 26112 | tf_op jit(solution)/shard_map/all_gather | solution.py:145
  32.5 91.5 %while.43 = (s32[]{:T(128)}, bf16[2048]{0:T(1024)(128)(2,1)S(1)}, s32[32]{0:T(128)S(1)}, f32[4096]{0:T(1024)S(1)}, f32[2048]{0:T(1024)S(1)}, /*index=5*/f32[4096...) while((s32[]{:T(128)}, bf16[2048]{0:T(1024)(128)(2,1)S(1)}, ...), condition=%wide.region_1.2_spmd.clone, body=%wide.region_0.1_spmd.clone.sunk | while | flops 24582 | bytes 57529 | solution.py:43
  35.3 0.7 dynamic_slice.136
  38.2 0.7 dynamic_slice.136
  41.0 0.7 dynamic_slice.136
  43.9 0.7 dynamic_slice.136
  46.7 0.7 dynamic_slice.136
  49.6 0.7 dynamic_slice.136
  52.5 0.7 dynamic_slice.136
  55.3 0.7 dynamic_slice.136
  58.2 0.7 dynamic_slice.136
  61.0 0.7 dynamic_slice.136
  78.2 0.7 dynamic_slice.136
  81.0 0.7 dynamic_slice.136
  83.9 0.7 dynamic_slice.136
  86.8 0.7 dynamic_slice.136
  124.5 3.5 %all-to-all-start = ((bf16[1,16,128]{2,0,1:T(2,128)(2,1)}), bf16[1,16,128]{2,0,1:T(2,128)(2,1)S(1)}, u32[]{:S(2)}, u32[]{:S(2)}) async-start(bf16[1,16,128]{2,0,1:T(2,128)(2,1)} %copy.16), calls=%async_computation | async-start | bytes 16384 | tf_op jit(solution)/shard_map/all_to_all | solution.py:150
  128.7 21.7 %all_gather.10 = f32[3,2048]{1,0:T(4,128)S(1)} all-gather(f32[3,128]{1,0:T(4,128)S(1)} %copy-done.5), channel_id=1, replica_groups=mesh['basin'=2,'recv'=8,'src'=2] {'recv','src'}, dimensions={1}, use_global_device_ids=true | all-gather | bytes 26112 | tf_op jit(solution)/shard_map/all_gather | solution.py:146
  152.0 17.4 %all-gather = f32[16,1,128]{2,1,0:T(1,128)S(1)} all-gather(f32[1,1,128]{2,1,0:T(1,128)S(1)} %bitcast.108), channel_id=1, replica_groups=mesh['basin'=2,'recv'=8,'src'=2] {'recv','src'}, dimensions={0}, use_global_device_ids=true | all-gather | bytes 8704 | tf_op jit(solution)/shard_map/all_gather | solution.py:147
  171.5 4.4 %collective-permute-done = bf16[16,128]{1,0:T(8,128)(2,1)S(1)} collective-permute-done((bf16[16,128]{1,0:T(8,128)(2,1)S(1)}, bf16[16,128]{1,0:T(8,128)(2,1)S(1)}, u32[]{:S(2)}, u32[]{:S(2)}) %collective-permute-start) | collective-permute-done | bytes 4128 | tf_op jit(solution)/shard_map/ppermute | solution.py:17
  175.9 5.1 %while.44 = (s32[]{:T(128)}, f32[16,1024]{1,0:T(8,128)S(1)}, s32[2]{0:T(128)S(1)}, bf16[16,256]{1,0:T(8,128)(2,1)S(1)}, f32[3,1024]{1,0:T(4,128)S(1)}, /*index=5...) while((s32[]{:T(128)}, f32[16,1024]{1,0:T(8,128)S(1)}, ...), condition=%wide.region_3.4_spmd.clone, body=%wide.region_2.3_spmd.clone.sunk | while | flops 8229127 | bytes 1284333 | solution.py:132
  177.6 0.8 convolution_add_fusion.2
  180.2 0.8 convolution_add_fusion.2
  181.7 6.1 %reduce-scatter.2.cloned.1.call-done = f32[16,4,1,128]{3,0,1,2:T(8,128)} async-done(((f32[16,4,2,128]{3,0,1,2:T(8,128)}), f32[16,4,1,128]{3,0,1,2:T(8,128)}) %reduce-scatter.2.cloned.1.call-update) | async-done | bytes 32784 | tf_op jit(solution)/shard_map/reduce_scatter | solution.py:195
  187.8 0.8 slice_select_fusion
  188.6 1.7 collective-permute-start.1
  190.3 2.1 %collective-permute-done.1 = f32[16,2,128]{2,0,1:T(8,128)S(1)} collective-permute-done((f32[16,2,128]{2,0,1:T(8,128)S(1)}, f32[16,2,128]{2,0,1:T(8,128)S(1)}, u32[]{:S(2)}, u32[]{:S(2)}) %collective-permute-start.1) | collective-permute-done | bytes 16416 | tf_op jit(solution)/shard_map/ppermute | solution.py:17
  192.4 1.7 collective-permute-start.2
  194.1 2.0 collective-permute-done.2
  196.7 1.5 while.42
  (204 shorter events, 25.5 us)
Async XLA Ops:
  7.9 0.7 copy-start.6
  31.8 0.7 copy-start.10
  124.5 46.0 %all-to-all-start = ((bf16[1,16,128]{2,0,1:T(2,128)(2,1)}), bf16[1,16,128]{2,0,1:T(2,128)(2,1)S(1)}, u32[]{:S(2)}, u32[]{:S(2)}) async-start(bf16[1,16,128]{2,0,1:T(2,128)(2,1)} %copy.16), calls=%async_computation | async-start | bytes 16384 | tf_op jit(solution)/shard_map/all_to_all | solution.py:150
  128.0 59.8 %reduce-scatter.2.cloned.1.call-start = ((), (), s32[]{:S(2)}) async-start(), calls=%async_computation.2 | async-start | bytes 98304 | tf_op jit(solution)/shard_map/reduce_scatter | solution.py:195
  128.1 0.7 copy-start.5
  150.5 0.7 copy-start.8
  150.5 0.7 copy-start.7
  151.3 0.7 copy-start.9
  170.6 0.7 copy-start.2
  171.3 4.6 %collective-permute-start = (bf16[16,128]{1,0:T(8,128)(2,1)S(1)}, bf16[16,128]{1,0:T(8,128)(2,1)S(1)}, u32[]{:S(2)}, u32[]{:S(2)}) collective-permute-start(bf16[16,128]{1,0:T(8,128)(2,1)S(1)} %get-tuple-element.374), channel_id=1, source_target_pairs={{0,8},{2,10},{4,12},{6,14},{8,0},{10,2},{12,4},{14,6},{1,9},{3,11}... | collective-permute-start | bytes 12296 | tf_op jit(solution)/shard_map/ppermute | solution.py:17
  187.8 4.5 %copy-start.1 = (f32[16,4,1,128]{3,0,1,2:T(8,128)S(1)}, f32[16,4,1,128]{3,0,1,2:T(8,128)}, u32[]{:S(2)}) copy-start(f32[16,4,1,128]{3,0,1,2:T(8,128)} %reduce-scatter.2.cloned.1.call-done) | copy-start | bytes 98308
  188.6 3.7 %collective-permute-start.1 = (f32[16,2,128]{2,0,1:T(8,128)S(1)}, f32[16,2,128]{2,0,1:T(8,128)S(1)}, u32[]{:S(2)}, u32[]{:S(2)}) collective-permute-start(f32[16,2,128]{2,0,1:T(8,128)S(1)} %slice_select_fusion), channel_id=1, source_target_pairs={{0,4},{2,6},{4,0},{6,2},{8,12},{10,14},{12,8},{14,10},{1,5},{3,7},... | collective-permute-start | bytes 49160 | tf_op jit(solution)/shard_map/ppermute | solution.py:17
  192.4 3.7 %collective-permute-start.2 = (f32[16,1,128]{2,0,1:T(8,128)S(1)}, f32[16,1,128]{2,0,1:T(8,128)S(1)}, u32[]{:S(2)}, u32[]{:S(2)}) collective-permute-start(f32[16,1,128]{2,0,1:T(8,128)S(1)} %slice_select_fusion.1), channel_id=1, source_target_pairs={{0,2},{2,0},{4,6},{6,4},{8,10},{10,8},{12,14},{14,12},{1,3},{3,1},... | collective-permute-start | bytes 24584 | tf_op jit(solution)/shard_map/ppermute | solution.py:17
  196.1 0.7 copy-start.4
  198.3 0.6 copy-start
  198.3 0.6 copy-start.3
Sparse Core Ops, SparseCore 0:
  181.8 5.9 reduce-scatter.1
where the time goes:
time: 207 us; the launch traced here: 206 us
  loops' own time  68.9 us (33%)
  blocking collectives  62.3 us (30%)
  local copies, waits for them, and re-layouts  31 us (15%)
  waiting for transfers between devices  14.5 us (7%)
  between operations  14.4 us (7%)
  starting transfers between devices  7 us (3%)
  other arithmetic  5.43 us (3%)
    another operation x1, loops' own time, profile_max(): best, unused = lax.scan(sweep, start, offsets)  67 us
    all_gather x1, blocking collectives, body(): lax.all_gather(positions, ('recv', 'src'), axis=1, tiled=True)  23.2 us
    all_gather x1, blocking collectives, body(): lax.all_gather(normals, ('recv', 'src'), axis=1, tiled=True)  21.7 us
    dynamic_slice x32, local copies, waits for them, and re-layouts, profile_max(): best, unused = lax.scan(sweep, start, offsets)  21.4 us
    all_gather x1, blocking collectives, body(): lax.all_gather(area, ('recv', 'src'), axis=0, tiled=True)  17.4 us
    ppermute x3, waiting for transfers between devices, partner(): return lax.ppermute(value, axis, pairs)  8.45 us
    reduce_scatter x1, waiting for transfers between devices, body(): lax.psum_scatter(partial_flux.reshape(epochs, 4, n_src, width), 'src', sc...  6.07 us
    unnamed x27, local copies, waits for them, and re-layouts  5.88 us
  transfers between devices with their start and end apart: 5, of which 4 were waited for; matrix products, arithmetic and copies ran while one was open for 1% of the time, Pallas kernels for 0%

commit v1 on v0

--- a/solution.py
+++ b/solution.py
@@ -9,6 +9,18 @@
 surface_gain = 0.1
 shade_width = 0.1
 reach_offset = 0.05
+
+
+def gather_by_bits(array, axis, dim):
+    ways, here, step = (lax.axis_size(axis), lax.axis_index(axis), array.shape[dim])
+    line, have = (array, 1)
+    while have < ways:
+        line = jnp.concatenate(
+            [line, lax.ppermute(line, axis, [(d, (d - have) % ways) for d in range(ways)])],
+            axis=dim,
+        )
+        have = 2 * have
+    return jnp.roll(line, here * step, axis=dim)
 
 
 def partner(value, axis, apart):
@@ -144,7 +156,7 @@
     all_pos, all_nrm, all_area = (
         lax.all_gather(positions, ("recv", "src"), axis=1, tiled=True),
         lax.all_gather(normals, ("recv", "src"), axis=1, tiled=True),
-        lax.all_gather(area, ("recv", "src"), axis=0, tiled=True),
+        gather_by_bits(area, ("recv", "src"), 0),
     )
     horizon = horizons(all_pos, samples)
     facet_horizon = lax.all_to_all(

time: 207 us -> 189 us (0.913)
  blocking collectives: 62.3 us -> 39.4 us
  waiting for transfers between devices: 14.5 us -> 28.9 us
  loops' own time: 68.9 us -> 57.4 us
  starting transfers between devices: 7 us -> 12.6 us
  local copies, waits for them, and re-layouts: 31 us -> 27.9 us
    all_gather x1 -> x0, blocking collectives: 17.4 us -> none  [body(): lax.all_gather(area, ('recv', 'src'), axis=0, tiled=True)]
    another operation x1, loops' own time: 67 us -> 55.2 us  [profile_max(): best, unused = lax.scan(sweep, start, offsets)]
    ppermute x0 -> x4, waiting for transfers between devices: none -> 11.6 us  [gather_by_bits(): lax.ppermute(line, axis, [(d, (d - have) % ways) for d in range(ways)])]
    ppermute x0 -> x4, starting transfers between devices: none -> 5.6 us  [gather_by_bits(): lax.ppermute(line, axis, [(d, (d - have) % ways) for d in range(ways)])]
    all_gather x1, blocking collectives: 23.2 us -> 17.7 us  [body(): lax.all_gather(positions, ('recv', 'src'), axis=1, tiled=True)]
    dynamic_slice x32, local copies, waits for them, and re-layouts: 21.4 us -> 18.5 us  [profile_max(): best, unused = lax.scan(sweep, start, offsets)]
    reduce_scatter x1, waiting for transfers between devices: 6.07 us -> 8.84 us  [body(): lax.psum_scatter(partial_flux.reshape(epochs, 4, n_src, width), 'src', sc...]
    unnamed x27 -> x36, local copies, waits for them, and re-layouts: 5.88 us -> 5.97 us
  transfers between devices with their start and end apart: 5 -> 9, of which waited for: 4 -> 7; matrix products, arithmetic and copies ran while one was open for 1% -> 12% of each run, Pallas kernels for 0% -> 0%
where the time goes in v1:
time: 189 us; the launch traced here: 188 us
  loops' own time  57.4 us (30%)
  blocking collectives  39.4 us (21%)
  waiting for transfers between devices  28.9 us (15%)
  local copies, waits for them, and re-layouts  27.9 us (15%)
  between operations  14.4 us (8%)
  starting transfers between devices  12.6 us (7%)
  other arithmetic  4.86 us (3%)
  matrix products  2.05 us (1%)
    another operation x1, loops' own time, profile_max(): best, unused = lax.scan(sweep, start, offsets)  55.2 us
    all_gather x1, blocking collectives, body(): lax.all_gather(normals, ('recv', 'src'), axis=1, tiled=True)  21.7 us
    dynamic_slice x32, local copies, waits for them, and re-layouts, profile_max(): best, unused = lax.scan(sweep, start, offsets)  18.5 us
    all_gather x1, blocking collectives, body(): lax.all_gather(positions, ('recv', 'src'), axis=1, tiled=True)  17.7 us
    ppermute x4, waiting for transfers between devices, gather_by_bits(): lax.ppermute(line, axis, [(d, (d - have) % ways) for d in range(ways)])  11.6 us
    reduce_scatter x1, waiting for transfers between devices, body(): lax.psum_scatter(partial_flux.reshape(epochs, 4, n_src, width), 'src', sc...  8.84 us
    ppermute x3, waiting for transfers between devices, partner(): return lax.ppermute(value, axis, pairs)  8.47 us
    unnamed x36, local copies, waits for them, and re-layouts  5.97 us
  transfers between devices with their start and end apart: 9, of which 7 were waited for; matrix products, arithmetic and copies ran while one was open for 12% of the time, Pallas kernels for 0%

profile of v1, /device:TPU:0, one launch (start us, length us, event | category | flops | bytes accessed | tf_op | source)
XLA Modules:
  0.0 187.6 jit_solution(13421242196986543495)
XLA Ops:
  7.2 0.7 copy.60
  7.9 5.5 %collective-permute-start.1 = (f32[128]{0:T(128)S(1)}, f32[128]{0:T(128)S(1)}, u32[]{:S(2)}, u32[]{:S(2)}) collective-permute-start(f32[128]{0:T(128)S(1)} %copy-done.6), channel_id=1, source_target_pairs={{0,15},{1,0},{2,1},{3,2},{4,3},{5,4},{6,5},{7,6},{8,7},{9,8},{10,9... | collective-permute-start | bytes 1544 | tf_op jit(solution)/shard_map/ppermute | solution.py:19
  13.4 0.7 copy-done.7
  14.1 17.7 %all_gather.6 = f32[3,2048]{1,0:T(4,128)S(1)} all-gather(f32[3,128]{1,0:T(4,128)S(1)} %copy-done.7), channel_id=1, replica_groups=mesh['basin'=2,'recv'=8,'src'=2] {'recv','src'}, dimensions={1}, use_global_device_ids=true | all-gather | bytes 26112 | tf_op jit(solution)/shard_map/all_gather | solution.py:157
  31.8 0.6 copy-done.10
  32.5 76.8 %while.43 = (s32[]{:T(128)}, bf16[2048]{0:T(1024)(128)(2,1)S(1)}, s32[32]{0:T(128)S(1)}, f32[4096]{0:T(1024)S(1)}, f32[2048]{0:T(1024)S(1)}, /*index=5*/f32[4096...) while((s32[]{:T(128)}, bf16[2048]{0:T(1024)(128)(2,1)S(1)}, ...), condition=%wide.region_1.2_spmd.clone, body=%wide.region_0.1_spmd.clone.sunk | while | flops 24582 | bytes 57529 | solution.py:55
  109.3 0.6 copy.16
  109.9 3.5 %all-to-all-start = ((bf16[1,16,128]{2,0,1:T(2,128)(2,1)}), bf16[1,16,128]{2,0,1:T(2,128)(2,1)S(1)}, u32[]{:S(2)}, u32[]{:S(2)}) async-start(bf16[1,16,128]{2,0,1:T(2,128)(2,1)} %copy.16), calls=%async_computation | async-start | bytes 16384 | tf_op jit(solution)/shard_map/all_to_all | solution.py:162
  113.6 0.6 copy-done.5
  114.2 21.7 %all_gather.7 = f32[3,2048]{1,0:T(4,128)S(1)} all-gather(f32[3,128]{1,0:T(4,128)S(1)} %copy-done.5), channel_id=1, replica_groups=mesh['basin'=2,'recv'=8,'src'=2] {'recv','src'}, dimensions={1}, use_global_device_ids=true | all-gather | bytes 26112 | tf_op jit(solution)/shard_map/all_gather | solution.py:158
  136.0 0.6 copy-done.9
  136.8 0.6 copy-done.8
  137.6 3.5 %collective-permute-done.2 = f32[256]{0:T(256)S(1)} collective-permute-done((f32[256]{0:T(256)S(1)}, f32[256]{0:T(256)S(1)}, u32[]{:S(2)}, u32[]{:S(2)}) %collective-permute-start.2) | collective-permute-done | bytes 1056 | tf_op jit(solution)/shard_map/ppermute | solution.py:19
  141.2 3.6 %collective-permute-done.3 = f32[512]{0:T(512)S(1)} collective-permute-done((f32[512]{0:T(512)S(1)}, f32[512]{0:T(512)S(1)}, u32[]{:S(2)}, u32[]{:S(2)}) %collective-permute-start.3) | collective-permute-done | bytes 2080 | tf_op jit(solution)/shard_map/ppermute | solution.py:19
  144.8 4.5 %collective-permute-done.4 = f32[1024]{0:T(1024)S(1)} collective-permute-done((f32[1024]{0:T(1024)S(1)}, f32[1024]{0:T(1024)S(1)}, u32[]{:S(2)}, u32[]{:S(2)}) %collective-permute-start.4) | collective-permute-done | bytes 4128 | tf_op jit(solution)/shard_map/ppermute | solution.py:19
  149.5 0.6 copy-done.2
  150.3 4.5 %collective-permute-done = bf16[16,128]{1,0:T(8,128)(2,1)S(1)} collective-permute-done((bf16[16,128]{1,0:T(8,128)(2,1)S(1)}, bf16[16,128]{1,0:T(8,128)(2,1)S(1)}, u32[]{:S(2)}, u32[]{:S(2)}) %collective-permute-start) | collective-permute-done | bytes 4128 | tf_op jit(solution)/shard_map/ppermute | solution.py:29
  154.8 5.2 %while.44 = (s32[]{:T(128)}, f32[16,1024]{1,0:T(8,128)S(1)}, s32[2]{0:T(128)S(1)}, bf16[16,256]{1,0:T(8,128)(2,1)S(1)}, f32[3,1024]{1,0:T(4,128)S(1)}, /*index=5...) while((s32[]{:T(128)}, f32[16,1024]{1,0:T(8,128)S(1)}, ...), condition=%wide.region_3.4_spmd.clone, body=%wide.region_2.3_spmd.clone.sunk | while | flops 8229127 | bytes 1284333 | solution.py:144
  154.8 0.6 dynamic_slice.144
  156.6 0.8 convolution_add_fusion.2
  157.4 0.6 dynamic_slice.144
  159.2 0.8 convolution_add_fusion.2
  160.1 0.7 copy.17
  160.8 8.8 %reduce-scatter.2.cloned.1.call-done = f32[16,4,1,128]{3,0,1,2:T(8,128)} async-done(((f32[16,4,2,128]{3,0,1,2:T(8,128)}), f32[16,4,1,128]{3,0,1,2:T(8,128)}) %reduce-scatter.2.cloned.1.call-update) | async-done | bytes 32784 | tf_op jit(solution)/shard_map/reduce_scatter | solution.py:207
  169.6 0.8 slice_select_fusion
  170.4 1.7 collective-permute-start.5
  172.1 2.0 %collective-permute-done.5 = f32[16,2,128]{2,0,1:T(8,128)S(1)} collective-permute-done((f32[16,2,128]{2,0,1:T(8,128)S(1)}, f32[16,2,128]{2,0,1:T(8,128)S(1)}, u32[]{:S(2)}, u32[]{:S(2)}) %collective-permute-start.5) | collective-permute-done | bytes 16416 | tf_op jit(solution)/shard_map/ppermute | solution.py:29
  174.2 1.8 collective-permute-start.6
  176.0 2.0 %collective-permute-done.6 = f32[16,1,128]{2,0,1:T(8,128)S(1)} collective-permute-done((f32[16,1,128]{2,0,1:T(8,128)S(1)}, f32[16,1,128]{2,0,1:T(8,128)S(1)}, u32[]{:S(2)}, u32[]{:S(2)}) %collective-permute-start.6) | collective-permute-done | bytes 8224 | tf_op jit(solution)/shard_map/ppermute | solution.py:29
  177.9 0.7 copy-done.4
  178.6 1.5 while.42
  180.1 0.6 copy-done
  (224 shorter events, 24.4 us)
Async XLA Ops:
  7.2 0.7 copy-start.6
  7.9 129.6 %collective-permute-start.1 = (f32[128]{0:T(128)S(1)}, f32[128]{0:T(128)S(1)}, u32[]{:S(2)}, u32[]{:S(2)}) collective-permute-start(f32[128]{0:T(128)S(1)} %copy-done.6), channel_id=1, source_target_pairs={{0,15},{1,0},{2,1},{3,2},{4,3},{5,4},{6,5},{7,6},{8,7},{9,8},{10,9... | collective-permute-start | bytes 1544 | tf_op jit(solution)/shard_map/ppermute | solution.py:19
  13.4 0.7 copy-start.7
  31.8 0.7 copy-start.10
  109.9 39.5 %all-to-all-start = ((bf16[1,16,128]{2,0,1:T(2,128)(2,1)}), bf16[1,16,128]{2,0,1:T(2,128)(2,1)S(1)}, u32[]{:S(2)}, u32[]{:S(2)}) async-start(bf16[1,16,128]{2,0,1:T(2,128)(2,1)} %copy.16), calls=%async_computation | async-start | bytes 16384 | tf_op jit(solution)/shard_map/all_to_all | solution.py:162
  113.4 56.2 %reduce-scatter.2.cloned.1.call-start = ((), (), s32[]{:S(2)}) async-start(), calls=%async_computation.2 | async-start | bytes 98304 | tf_op jit(solution)/shard_map/reduce_scatter | solution.py:207
  113.5 0.7 copy-start.5
  136.0 0.7 copy-start.9
  136.8 0.7 copy-start.8
  137.5 3.6 %collective-permute-start.2 = (f32[256]{0:T(256)S(1)}, f32[256]{0:T(256)S(1)}, u32[]{:S(2)}, u32[]{:S(2)}) collective-permute-start(f32[256]{0:T(256)S(1)} %pad_maximum_fusion.6), channel_id=1, source_target_pairs={{0,14},{1,15},{2,0},{3,1},{4,2},{5,3},{6,4},{7,5},{8,6},{9,7},{10,... | collective-permute-start | bytes 3080 | tf_op jit(solution)/shard_map/ppermute | solution.py:19
  141.1 3.6 %collective-permute-start.3 = (f32[512]{0:T(512)S(1)}, f32[512]{0:T(512)S(1)}, u32[]{:S(2)}, u32[]{:S(2)}) collective-permute-start(f32[512]{0:T(512)S(1)} %pad_maximum_fusion.5), channel_id=1, source_target_pairs={{0,12},{1,13},{2,14},{3,15},{4,0},{5,1},{6,2},{7,3},{8,4},{9,5},{1... | collective-permute-start | bytes 6152 | tf_op jit(solution)/shard_map/ppermute | solution.py:19
  144.7 4.6 %collective-permute-start.4 = (f32[1024]{0:T(1024)S(1)}, f32[1024]{0:T(1024)S(1)}, u32[]{:S(2)}, u32[]{:S(2)}) collective-permute-start(f32[1024]{0:T(1024)S(1)} %pad_maximum_fusion.4), channel_id=1, source_target_pairs={{0,8},{1,9},{2,10},{3,11},{4,12},{5,13},{6,14},{7,15},{8,0},{9,1},... | collective-permute-start | bytes 12296 | tf_op jit(solution)/shard_map/ppermute | solution.py:19
  149.5 0.7 copy-start.2
  150.2 4.6 %collective-permute-start = (bf16[16,128]{1,0:T(8,128)(2,1)S(1)}, bf16[16,128]{1,0:T(8,128)(2,1)S(1)}, u32[]{:S(2)}, u32[]{:S(2)}) collective-permute-start(bf16[16,128]{1,0:T(8,128)(2,1)S(1)} %get-tuple-element.374), channel_id=1, source_target_pairs={{0,8},{2,10},{4,12},{6,14},{8,0},{10,2},{12,4},{14,6},{1,9},{3,11}... | collective-permute-start | bytes 12296 | tf_op jit(solution)/shard_map/ppermute | solution.py:29
  169.6 4.5 %copy-start.1 = (f32[16,4,1,128]{3,0,1,2:T(8,128)S(1)}, f32[16,4,1,128]{3,0,1,2:T(8,128)}, u32[]{:S(2)}) copy-start(f32[16,4,1,128]{3,0,1,2:T(8,128)} %reduce-scatter.2.cloned.1.call-done) | copy-start | bytes 98308
  170.4 3.7 %collective-permute-start.5 = (f32[16,2,128]{2,0,1:T(8,128)S(1)}, f32[16,2,128]{2,0,1:T(8,128)S(1)}, u32[]{:S(2)}, u32[]{:S(2)}) collective-permute-start(f32[16,2,128]{2,0,1:T(8,128)S(1)} %slice_select_fusion), channel_id=1, source_target_pairs={{0,4},{2,6},{4,0},{6,2},{8,12},{10,14},{12,8},{14,10},{1,5},{3,7},... | collective-permute-start | bytes 49160 | tf_op jit(solution)/shard_map/ppermute | solution.py:29
  174.2 3.7 %collective-permute-start.6 = (f32[16,1,128]{2,0,1:T(8,128)S(1)}, f32[16,1,128]{2,0,1:T(8,128)S(1)}, u32[]{:S(2)}, u32[]{:S(2)}) collective-permute-start(f32[16,1,128]{2,0,1:T(8,128)S(1)} %slice_select_fusion.1), channel_id=1, source_target_pairs={{0,2},{2,0},{4,6},{6,4},{8,10},{10,8},{12,14},{14,12},{1,3},{3,1},... | collective-permute-start | bytes 24584 | tf_op jit(solution)/shard_map/ppermute | solution.py:29
  177.9 0.7 copy-start.4
  180.1 0.6 copy-start
  180.1 0.6 copy-start.3
Sparse Core Ops, SparseCore 0:
  160.9 8.7 reduce-scatter.1
